TPU v7x, 32 devices: a whole 2x2x4 slice. The times are simulated.
32 devices in a mesh: gx: 8 (over y, x, core), gy: 4 (over z).
Axes of the slice: x: 2, y: 2, z: 4, core: 2. Of those that a mesh axis runs over, the one named last changes fastest.
Arguments:
- snapshots: bfloat16 [2, 1, 256, 256, 512], P(None, None, 'gx', 'gy'), may hold values from -12 to 12
- start: float32 [1, 32, 256, 256], P(None, None, 'gx', 'gy'), may hold values from -6 to 6
Outputs:
- basis_field: float32 [1, 32, 256, 256], P(None, None, 'gx', 'gy')
- phi: float32 [1, 2, 32, 32], replicated
All inputs are finite; a program needn't handle non-finite values.
Results may differ from a plain program's by a relative error of at most 0.0005.
Values may be sent and summed in bfloat16 or wider, within the bound.
A program may use at most 64 MiB of HBM per device.

v0:
```python
import jax
import jax.numpy as jnp
from jax import lax
from jax.sharding import PartitionSpec as P

ITERS = 4
precise = lax.Precision.HIGHEST


def swapped(x, axis, apart):
    return lax.ppermute(x, axis, [(i, i ^ 1 << apart) for i in range(lax.axis_size(axis))])


def passed_along(block, axis, distance):
    devices = range(lax.axis_size(axis))
    route = [(i - distance, i) for i in devices if i - distance in devices]
    return lax.ppermute(block, axis, route)


def inverse_factor(matrix):
    factor = jnp.linalg.cholesky(matrix)
    identity = jnp.broadcast_to(jnp.eye(matrix.shape[-1], dtype=matrix.dtype), matrix.shape)
    inverse = lax.linalg.triangular_solve(factor, identity, left_side=True, lower=True)
    return (factor, inverse)


def apply_inverse(inverse, right_side):
    return jnp.einsum("...kj,...jm->...km", inverse, right_side, precision=precise)


def shift_solve(inverse, right_matrix):
    inner = apply_inverse(inverse, right_matrix)
    return apply_inverse(jnp.swapaxes(inverse, -1, -2), inner)


def project(local_side):
    return lax.psum(local_side, ("gx", "gy"))


def gram_of(grown):
    return jnp.einsum("fkm,fjm->fkj", grown, grown, precision=precise)


def pair_grams(plus_terms, minus_terms):
    left_matrix = jnp.einsum("fkab,fjab->fkj", plus_terms, plus_terms, precision=precise)
    right_matrix = jnp.einsum("fkab,fjab->fkj", plus_terms, minus_terms, precision=precise)
    return (left_matrix, right_matrix)


def mirror_fields(stacked, rows, cols):
    moved = stacked
    for bit_number in range(lax.axis_size("gx").bit_length() - 1):
        moved = swapped(moved, "gx", bit_number)
    for bit_number in range(lax.axis_size("gy").bit_length() - 1):
        moved = swapped(moved, "gy", bit_number)
    lead = moved.shape[:-1]
    turned = moved.reshape(lead + (rows, cols))[..., ::-1, ::-1]
    return turned.reshape(moved.shape)


def shift_terms(field):
    rows = field.shape[2]
    cols = field.shape[3]
    below = passed_along(field[:, :, :1, :], "gx", -1)
    beside = passed_along(field[:, :, :, :1], "gy", -1)
    last_row_device = lax.axis_index("gx") == lax.axis_size("gx") - 1
    last_col_device = lax.axis_index("gy") == lax.axis_size("gy") - 1
    row_weight = jnp.where((jnp.arange(rows) == rows - 1) & last_row_device, 0.0, 1.0).astype(
        jnp.float32
    )
    col_weight = jnp.where((jnp.arange(cols) == cols - 1) & last_col_device, 0.0, 1.0).astype(
        jnp.float32
    )
    row_extended = jnp.concatenate([field, below], axis=2)
    col_extended = jnp.concatenate([field, beside], axis=3)
    row_plus = (row_extended[:, :, 1:] + row_extended[:, :, :-1]) * row_weight[:, None]
    row_minus = row_extended[:, :, 1:] - row_extended[:, :, :-1]
    col_plus = (col_extended[:, :, :, 1:] + col_extended[:, :, :, :-1]) * col_weight
    col_minus = col_extended[:, :, :, 1:] - col_extended[:, :, :, :-1]
    row_lhs, row_rhs = pair_grams(row_plus, row_minus)
    col_lhs, col_rhs = pair_grams(col_plus, col_minus)
    return (row_lhs, row_rhs, col_lhs, col_rhs)


def body(snapshots, start):
    frames, basis_count, rows, cols = start.shape
    upper_half = lax.axis_index("gx") < lax.axis_size("gx") // 2
    start_flat = start.reshape(frames, basis_count, rows * cols)
    own = snapshots.astype(jnp.float32).reshape(2, frames, rows * cols, -1)

    def local_side(weights, weights_mirror):
        p_real = jnp.einsum("fkm,fms->fks", weights, own[0], precision=precise)
        p_imag = jnp.einsum("fkm,fms->fks", weights, own[1], precision=precise)
        q_real = jnp.einsum("fkm,fms->fks", weights_mirror, own[0], precision=precise)
        q_imag = jnp.einsum("fkm,fms->fks", weights_mirror, own[1], precision=precise)
        first = jnp.where(upper_half, p_real - q_imag, p_imag + q_real)
        second = jnp.where(upper_half, -p_imag - q_real, p_real - q_imag)
        return jnp.concatenate([first, second], axis=-1)

    start_mirror = mirror_fields(start_flat[None], rows, cols)[0]
    basis = start_flat
    basis_mirror = start_mirror
    for step_index in range(ITERS):
        side = project(local_side(basis, basis_mirror))
        half = side.shape[-1] // 2
        side_first = side[..., :half]
        side_second = side[..., half:]
        g_real = jnp.einsum("fks,fms->fkm", side_first, own[0], precision=precise) - jnp.einsum(
            "fks,fms->fkm", side_second, own[1], precision=precise
        )
        g_imag = jnp.einsum("fks,fms->fkm", side_first, own[1], precision=precise) + jnp.einsum(
            "fks,fms->fkm", side_second, own[0], precision=precise
        )
        moved = mirror_fields(jnp.stack([g_real, g_imag]), rows, cols)
        grown = jnp.where(upper_half, g_real + moved[0], g_imag - moved[1])
        grown_mirror = jnp.where(upper_half, moved[1] - g_imag, moved[0] + g_real)
        grown, grown_mirror = (grown, grown_mirror)
        gram = lax.psum(gram_of(grown), ("gx", "gy"))
        factor, inverse = inverse_factor(gram)
        basis = apply_inverse(inverse, grown)
        basis_mirror = apply_inverse(inverse, grown_mirror)
    field = basis.reshape(frames, basis_count, rows, cols)
    local_terms = shift_terms(field)
    row_lhs, row_rhs, col_lhs, col_rhs = lax.psum(
        (local_terms[0], local_terms[1], local_terms[2], local_terms[3]), ("gx", "gy")
    )
    factors, inverses = inverse_factor(jnp.stack([row_lhs, col_lhs]))
    phi = jnp.swapaxes(shift_solve(inverses, jnp.stack([row_rhs, col_rhs])), 0, 1)
    return (field, phi)


def solution(mesh):
    return jax.shard_map(
        body,
        mesh=mesh,
        in_specs=(P(None, None, "gx", "gy", None), P(None, None, "gx", "gy")),
        out_specs=(P(None, None, "gx", "gy"), P()),
        check_vma=False,
    )
```

profile of v0, /device:TPU:0, one launch (start us, length us, event | category | flops | bytes accessed | tf_op | source)
XLA Modules:
  0.0 1151.4 jit_solution(10792632579092109949)
XLA Ops:
  53.8 125.0 %all-reduce.6.cloned.1.call-done = f32[1,32,1024]{2,1,0:T(8,128)} async-done(((f32[1,32,1024]{2,1,0:T(8,128)}), f32[1,32,1024]{2,1,0:T(8,128)}) %all-reduce.6.cloned.1.call-update) | async-done | bytes 131088 | tf_op jit(solution)/shard_map/psum | solution.py:37
  191.0 12.5 %collective-permute-done.6 = f32[2,1,32,2048]{3,2,1,0:T(8,128)S(1)} collective-permute-done((f32[2,1,32,2048]{3,2,1,0:T(8,128)S(1)}, f32[2,1,32,2048]{3,2,1,0:T(8,128)S(1)}, u32[]{:S(2)}, u32[]{:S(2)}) %collective-permute-start.6) | collective-permute-done | bytes 524320 | tf_op jit(solution)/shard_map/ppermute | solution.py:11
  204.9 11.6 %collective-permute-done.7 = f32[2,1,32,2048]{3,2,1,0:T(8,128)S(1)} collective-permute-done((f32[2,1,32,2048]{3,2,1,0:T(8,128)S(1)}, f32[2,1,32,2048]{3,2,1,0:T(8,128)S(1)}, u32[]{:S(2)}, u32[]{:S(2)}) %collective-permute-start.7) | collective-permute-done | bytes 524320 | tf_op jit(solution)/shard_map/ppermute | solution.py:11
  218.0 10.8 collective-permute-done.8
  230.3 22.1 %collective-permute-done.9 = f32[2,1,32,2048]{3,2,1,0:T(8,128)S(1)} collective-permute-done((f32[2,1,32,2048]{3,2,1,0:T(8,128)S(1)}, f32[2,1,32,2048]{3,2,1,0:T(8,128)S(1)}, u32[]{:S(2)}, u32[]{:S(2)}) %collective-permute-start.9) | collective-permute-done | bytes 524320 | tf_op jit(solution)/shard_map/ppermute | solution.py:11
  259.4 38.0 %psum.85 = f32[1,32,32]{1,2,0:T(8,128)S(1)} all-reduce(f32[1,32,32]{1,2,0:T(8,128)S(1)} %convolution_bitcast_fusion.10), channel_id=1, replica_groups=mesh['gx'=8,'gy'=4] {'gx','gy'}, use_global_device_ids=true, to_apply=%region_1.2 | all-reduce | flops 1024 | bytes 8192 | tf_op jit(solution)/shard_map/psum | solution.py:118
  310.2 125.8 %all-reduce.8.cloned.1.call-done = f32[1,32,1024]{2,1,0:T(8,128)} async-done(((f32[1,32,1024]{2,1,0:T(8,128)}), f32[1,32,1024]{2,1,0:T(8,128)}) %all-reduce.8.cloned.1.call-update) | async-done | bytes 131088 | tf_op jit(solution)/shard_map/psum | solution.py:37
  448.2 12.5 %collective-permute-done.11 = f32[2,1,32,2048]{3,2,1,0:T(8,128)S(1)} collective-permute-done((f32[2,1,32,2048]{3,2,1,0:T(8,128)S(1)}, f32[2,1,32,2048]{3,2,1,0:T(8,128)S(1)}, u32[]{:S(2)}, u32[]{:S(2)}) %collective-permute-start.11) | collective-permute-done | bytes 524320 | tf_op jit(solution)/shard_map/ppermute | solution.py:11
  462.1 11.6 %collective-permute-done.12 = f32[2,1,32,2048]{3,2,1,0:T(8,128)S(1)} collective-permute-done((f32[2,1,32,2048]{3,2,1,0:T(8,128)S(1)}, f32[2,1,32,2048]{3,2,1,0:T(8,128)S(1)}, u32[]{:S(2)}, u32[]{:S(2)}) %collective-permute-start.12) | collective-permute-done | bytes 524320 | tf_op jit(solution)/shard_map/ppermute | solution.py:11
  487.5 22.1 %collective-permute-done.14 = f32[2,1,32,2048]{3,2,1,0:T(8,128)S(1)} collective-permute-done((f32[2,1,32,2048]{3,2,1,0:T(8,128)S(1)}, f32[2,1,32,2048]{3,2,1,0:T(8,128)S(1)}, u32[]{:S(2)}, u32[]{:S(2)}) %collective-permute-start.14) | collective-permute-done | bytes 524320 | tf_op jit(solution)/shard_map/ppermute | solution.py:11
  516.6 38.1 %psum.87 = f32[1,32,32]{1,2,0:T(8,128)S(1)} all-reduce(f32[1,32,32]{1,2,0:T(8,128)S(1)} %convolution_bitcast_fusion.9), channel_id=1, replica_groups=mesh['gx'=8,'gy'=4] {'gx','gy'}, use_global_device_ids=true, to_apply=%region_5.8 | all-reduce | flops 1024 | bytes 8192 | tf_op jit(solution)/shard_map/psum | solution.py:118
  567.5 125.8 %all-reduce.10.cloned.1.call-done = f32[1,32,1024]{2,1,0:T(8,128)} async-done(((f32[1,32,1024]{2,1,0:T(8,128)}), f32[1,32,1024]{2,1,0:T(8,128)}) %all-reduce.10.cloned.1.call-update) | async-done | bytes 131088 | tf_op jit(solution)/shard_map/psum | solution.py:37
  705.4 12.5 %collective-permute-done.16 = f32[2,1,32,2048]{3,2,1,0:T(8,128)S(1)} collective-permute-done((f32[2,1,32,2048]{3,2,1,0:T(8,128)S(1)}, f32[2,1,32,2048]{3,2,1,0:T(8,128)S(1)}, u32[]{:S(2)}, u32[]{:S(2)}) %collective-permute-start.16) | collective-permute-done | bytes 524320 | tf_op jit(solution)/shard_map/ppermute | solution.py:11
  719.4 11.6 %collective-permute-done.17 = f32[2,1,32,2048]{3,2,1,0:T(8,128)S(1)} collective-permute-done((f32[2,1,32,2048]{3,2,1,0:T(8,128)S(1)}, f32[2,1,32,2048]{3,2,1,0:T(8,128)S(1)}, u32[]{:S(2)}, u32[]{:S(2)}) %collective-permute-start.17) | collective-permute-done | bytes 524320 | tf_op jit(solution)/shard_map/ppermute | solution.py:11
  732.5 10.8 collective-permute-done.18
  744.7 22.1 %collective-permute-done.19 = f32[2,1,32,2048]{3,2,1,0:T(8,128)S(1)} collective-permute-done((f32[2,1,32,2048]{3,2,1,0:T(8,128)S(1)}, f32[2,1,32,2048]{3,2,1,0:T(8,128)S(1)}, u32[]{:S(2)}, u32[]{:S(2)}) %collective-permute-start.19) | collective-permute-done | bytes 524320 | tf_op jit(solution)/shard_map/ppermute | solution.py:11
  773.8 38.2 %psum.89 = f32[1,32,32]{1,2,0:T(8,128)S(1)} all-reduce(f32[1,32,32]{1,2,0:T(8,128)S(1)} %convolution_bitcast_fusion.8), channel_id=1, replica_groups=mesh['gx'=8,'gy'=4] {'gx','gy'}, use_global_device_ids=true, to_apply=%region_7.10 | all-reduce | flops 1024 | bytes 8192 | tf_op jit(solution)/shard_map/psum | solution.py:118
  824.9 125.8 %all-reduce.12.cloned.1.call-done = f32[1,32,1024]{2,1,0:T(8,128)} async-done(((f32[1,32,1024]{2,1,0:T(8,128)}), f32[1,32,1024]{2,1,0:T(8,128)}) %all-reduce.12.cloned.1.call-update) | async-done | bytes 131088 | tf_op jit(solution)/shard_map/psum | solution.py:37
  962.8 12.5 %collective-permute-done.21 = f32[2,1,32,2048]{3,2,1,0:T(8,128)S(1)} collective-permute-done((f32[2,1,32,2048]{3,2,1,0:T(8,128)S(1)}, f32[2,1,32,2048]{3,2,1,0:T(8,128)S(1)}, u32[]{:S(2)}, u32[]{:S(2)}) %collective-permute-start.21) | collective-permute-done | bytes 524320 | tf_op jit(solution)/shard_map/ppermute | solution.py:11
  976.8 11.6 %collective-permute-done.22 = f32[2,1,32,2048]{3,2,1,0:T(8,128)S(1)} collective-permute-done((f32[2,1,32,2048]{3,2,1,0:T(8,128)S(1)}, f32[2,1,32,2048]{3,2,1,0:T(8,128)S(1)}, u32[]{:S(2)}, u32[]{:S(2)}) %collective-permute-start.22) | collective-permute-done | bytes 524320 | tf_op jit(solution)/shard_map/ppermute | solution.py:11
  1002.2 22.0 %collective-permute-done.24 = f32[2,1,32,2048]{3,2,1,0:T(8,128)S(1)} collective-permute-done((f32[2,1,32,2048]{3,2,1,0:T(8,128)S(1)}, f32[2,1,32,2048]{3,2,1,0:T(8,128)S(1)}, u32[]{:S(2)}, u32[]{:S(2)}) %collective-permute-start.24) | collective-permute-done | bytes 524320 | tf_op jit(solution)/shard_map/ppermute | solution.py:11
  1026.1 38.0 %psum.91 = f32[1,32,32]{1,2,0:T(8,128)S(1)} all-reduce(f32[1,32,32]{1,2,0:T(8,128)S(1)} %convolution_bitcast_fusion.7), channel_id=1, replica_groups=mesh['gx'=8,'gy'=4] {'gx','gy'}, use_global_device_ids=true, to_apply=%region_9.12 | all-reduce | flops 1024 | bytes 8192 | tf_op jit(solution)/shard_map/psum | solution.py:118
  1075.8 12.2 %collective-permute-done.26 = f32[1,32,32,1]{3,1,2,0:T(8,128)S(1)} collective-permute-done((f32[1,32,32,1]{3,1,2,0:T(8,128)S(1)}, f32[1,32,32,1]{3,1,2,0:T(8,128)S(1)}, u32[]{:S(2)}, u32[]{:S(2)}) %collective-permute-start.26) | collective-permute-done | bytes 4128 | tf_op jit(solution)/shard_map/ppermute | solution.py:17
  1091.3 40.9 %all-reduce = (f32[1,1,32,32]{2,3,1,0:T(8,128)S(1)}, f32[1,1,32,32]{2,3,1,0:T(8,128)S(1)}, f32[1,1,32,32]{3,2,1,0:T(8,128)S(1)}, f32[1,1,32,32]{3,2,1,0:T(8,128)S(1)}) all-reduce(f32[1,1,32,32]{2,3,1,0:T(8,128)S(1)} %convolution_bitcast_fusion.5, ...), channel_id=1, replica_groups=mesh['gx'=8,'gy'=4] {'gx','gy'}, use_global_device_ids=true, to_apply=%region_10.13 | all-reduce | flops 4096 | bytes 32768 | tf_op jit(solution)/shard_map/psum | solution.py:124
  (215 shorter events, 222.4 us)
Async XLA Ops:
  7.2 171.7 %all-reduce.6.cloned.1.call-start = ((), (), s32[]{:S(2)}) async-start(), calls=%async_computation | async-start | bytes 262144 | tf_op jit(solution)/shard_map/psum | solution.py:37
  10.2 9.5 collective-permute-start.1
  34.3 12.6 %collective-permute-start.4 = (f32[1,1,32,2048]{3,2,1,0:T(8,128)S(1)}, f32[1,1,32,2048]{3,2,1,0:T(8,128)S(1)}, u32[]{:S(2)}, u32[]{:S(2)}) collective-permute-start(f32[1,1,32,2048]{3,2,1,0:T(8,128)S(1)} %collective-permute-done.3), channel_id=1, source_target_pairs={{0,2},{1,3},{2,0},{3,1},{4,6},{5,7},{6,4},{7,5},{8,10},{9,11},{10,... | collective-permute-start | bytes 786440 | tf_op jit(solution)/shard_map/ppermute | solution.py:11
  53.8 382.3 %all-reduce.8.cloned.1.call-start = ((), (), s32[]{:S(2)}) async-start(), calls=%async_computation.1 | async-start | bytes 262144 | tf_op jit(solution)/shard_map/psum | solution.py:37
  189.5 14.0 %collective-permute-start.6 = (f32[2,1,32,2048]{3,2,1,0:T(8,128)S(1)}, f32[2,1,32,2048]{3,2,1,0:T(8,128)S(1)}, u32[]{:S(2)}, u32[]{:S(2)}) collective-permute-start(f32[2,1,32,2048]{3,2,1,0:T(8,128)S(1)} %collective-permute-done.5), channel_id=1, source_target_pairs={{0,8},{4,12},{8,0},{12,4},{16,24},{20,28},{24,16},{28,20},{1,9},{5... | collective-permute-start | bytes 1572872 | tf_op jit(solution)/shard_map/ppermute | solution.py:11
  203.5 13.1 %collective-permute-start.7 = (f32[2,1,32,2048]{3,2,1,0:T(8,128)S(1)}, f32[2,1,32,2048]{3,2,1,0:T(8,128)S(1)}, u32[]{:S(2)}, u32[]{:S(2)}) collective-permute-start(f32[2,1,32,2048]{3,2,1,0:T(8,128)S(1)} %collective-permute-done.6), channel_id=1, source_target_pairs={{0,16},{4,20},{8,24},{12,28},{16,0},{20,4},{24,8},{28,12},{1,17},{... | collective-permute-start | bytes 1572872 | tf_op jit(solution)/shard_map/ppermute | solution.py:11
  216.6 12.3 %collective-permute-start.8 = (f32[2,1,32,2048]{3,2,1,0:T(8,128)S(1)}, f32[2,1,32,2048]{3,2,1,0:T(8,128)S(1)}, u32[]{:S(2)}, u32[]{:S(2)}) collective-permute-start(f32[2,1,32,2048]{3,2,1,0:T(8,128)S(1)} %collective-permute-done.7), channel_id=1, source_target_pairs={{0,1},{1,0},{2,3},{3,2},{4,5},{5,4},{6,7},{7,6},{8,9},{9,8},{10,11... | collective-permute-start | bytes 1572872 | tf_op jit(solution)/shard_map/ppermute | solution.py:11
  228.8 23.5 %collective-permute-start.9 = (f32[2,1,32,2048]{3,2,1,0:T(8,128)S(1)}, f32[2,1,32,2048]{3,2,1,0:T(8,128)S(1)}, u32[]{:S(2)}, u32[]{:S(2)}) collective-permute-start(f32[2,1,32,2048]{3,2,1,0:T(8,128)S(1)} %collective-permute-done.8), channel_id=1, source_target_pairs={{0,2},{1,3},{2,0},{3,1},{4,6},{5,7},{6,4},{7,5},{8,10},{9,11},{10,... | collective-permute-start | bytes 1572872 | tf_op jit(solution)/shard_map/ppermute | solution.py:11
  310.2 383.1 %all-reduce.10.cloned.1.call-start = ((), (), s32[]{:S(2)}) async-start(), calls=%async_computation.2 | async-start | bytes 262144 | tf_op jit(solution)/shard_map/psum | solution.py:37
  446.7 14.0 %collective-permute-start.11 = (f32[2,1,32,2048]{3,2,1,0:T(8,128)S(1)}, f32[2,1,32,2048]{3,2,1,0:T(8,128)S(1)}, u32[]{:S(2)}, u32[]{:S(2)}) collective-permute-start(f32[2,1,32,2048]{3,2,1,0:T(8,128)S(1)} %collective-permute-done.10), channel_id=1, source_target_pairs={{0,8},{4,12},{8,0},{12,4},{16,24},{20,28},{24,16},{28,20},{1,9},{5... | collective-permute-start | bytes 1572872 | tf_op jit(solution)/shard_map/ppermute | solution.py:11
  460.7 13.1 %collective-permute-start.12 = (f32[2,1,32,2048]{3,2,1,0:T(8,128)S(1)}, f32[2,1,32,2048]{3,2,1,0:T(8,128)S(1)}, u32[]{:S(2)}, u32[]{:S(2)}) collective-permute-start(f32[2,1,32,2048]{3,2,1,0:T(8,128)S(1)} %collective-permute-done.11), channel_id=1, source_target_pairs={{0,16},{4,20},{8,24},{12,28},{16,0},{20,4},{24,8},{28,12},{1,17},{... | collective-permute-start | bytes 1572872 | tf_op jit(solution)/shard_map/ppermute | solution.py:11
  473.8 12.3 %collective-permute-start.13 = (f32[2,1,32,2048]{3,2,1,0:T(8,128)S(1)}, f32[2,1,32,2048]{3,2,1,0:T(8,128)S(1)}, u32[]{:S(2)}, u32[]{:S(2)}) collective-permute-start(f32[2,1,32,2048]{3,2,1,0:T(8,128)S(1)} %collective-permute-done.12), channel_id=1, source_target_pairs={{0,1},{1,0},{2,3},{3,2},{4,5},{5,4},{6,7},{7,6},{8,9},{9,8},{10,11... | collective-permute-start | bytes 1572872 | tf_op jit(solution)/shard_map/ppermute | solution.py:11
  486.0 23.5 %collective-permute-start.14 = (f32[2,1,32,2048]{3,2,1,0:T(8,128)S(1)}, f32[2,1,32,2048]{3,2,1,0:T(8,128)S(1)}, u32[]{:S(2)}, u32[]{:S(2)}) collective-permute-start(f32[2,1,32,2048]{3,2,1,0:T(8,128)S(1)} %collective-permute-done.13), channel_id=1, source_target_pairs={{0,2},{1,3},{2,0},{3,1},{4,6},{5,7},{6,4},{7,5},{8,10},{9,11},{10,... | collective-permute-start | bytes 1572872 | tf_op jit(solution)/shard_map/ppermute | solution.py:11
  567.5 383.3 %all-reduce.12.cloned.1.call-start = ((), (), s32[]{:S(2)}) async-start(), calls=%async_computation.3 | async-start | bytes 262144 | tf_op jit(solution)/shard_map/psum | solution.py:37
  703.9 14.0 %collective-permute-start.16 = (f32[2,1,32,2048]{3,2,1,0:T(8,128)S(1)}, f32[2,1,32,2048]{3,2,1,0:T(8,128)S(1)}, u32[]{:S(2)}, u32[]{:S(2)}) collective-permute-start(f32[2,1,32,2048]{3,2,1,0:T(8,128)S(1)} %collective-permute-done.15), channel_id=1, source_target_pairs={{0,8},{4,12},{8,0},{12,4},{16,24},{20,28},{24,16},{28,20},{1,9},{5... | collective-permute-start | bytes 1572872 | tf_op jit(solution)/shard_map/ppermute | solution.py:11
  717.9 13.1 %collective-permute-start.17 = (f32[2,1,32,2048]{3,2,1,0:T(8,128)S(1)}, f32[2,1,32,2048]{3,2,1,0:T(8,128)S(1)}, u32[]{:S(2)}, u32[]{:S(2)}) collective-permute-start(f32[2,1,32,2048]{3,2,1,0:T(8,128)S(1)} %collective-permute-done.16), channel_id=1, source_target_pairs={{0,16},{4,20},{8,24},{12,28},{16,0},{20,4},{24,8},{28,12},{1,17},{... | collective-permute-start | bytes 1572872 | tf_op jit(solution)/shard_map/ppermute | solution.py:11
  731.0 12.3 %collective-permute-start.18 = (f32[2,1,32,2048]{3,2,1,0:T(8,128)S(1)}, f32[2,1,32,2048]{3,2,1,0:T(8,128)S(1)}, u32[]{:S(2)}, u32[]{:S(2)}) collective-permute-start(f32[2,1,32,2048]{3,2,1,0:T(8,128)S(1)} %collective-permute-done.17), channel_id=1, source_target_pairs={{0,1},{1,0},{2,3},{3,2},{4,5},{5,4},{6,7},{7,6},{8,9},{9,8},{10,11... | collective-permute-start | bytes 1572872 | tf_op jit(solution)/shard_map/ppermute | solution.py:11
  743.3 23.5 %collective-permute-start.19 = (f32[2,1,32,2048]{3,2,1,0:T(8,128)S(1)}, f32[2,1,32,2048]{3,2,1,0:T(8,128)S(1)}, u32[]{:S(2)}, u32[]{:S(2)}) collective-permute-start(f32[2,1,32,2048]{3,2,1,0:T(8,128)S(1)} %collective-permute-done.18), channel_id=1, source_target_pairs={{0,2},{1,3},{2,0},{3,1},{4,6},{5,7},{6,4},{7,5},{8,10},{9,11},{10,... | collective-permute-start | bytes 1572872 | tf_op jit(solution)/shard_map/ppermute | solution.py:11
  961.4 14.0 %collective-permute-start.21 = (f32[2,1,32,2048]{3,2,1,0:T(8,128)S(1)}, f32[2,1,32,2048]{3,2,1,0:T(8,128)S(1)}, u32[]{:S(2)}, u32[]{:S(2)}) collective-permute-start(f32[2,1,32,2048]{3,2,1,0:T(8,128)S(1)} %collective-permute-done.20), channel_id=1, source_target_pairs={{0,8},{4,12},{8,0},{12,4},{16,24},{20,28},{24,16},{28,20},{1,9},{5... | collective-permute-start | bytes 1572872 | tf_op jit(solution)/shard_map/ppermute | solution.py:11
  975.3 13.1 %collective-permute-start.22 = (f32[2,1,32,2048]{3,2,1,0:T(8,128)S(1)}, f32[2,1,32,2048]{3,2,1,0:T(8,128)S(1)}, u32[]{:S(2)}, u32[]{:S(2)}) collective-permute-start(f32[2,1,32,2048]{3,2,1,0:T(8,128)S(1)} %collective-permute-done.21), channel_id=1, source_target_pairs={{0,16},{4,20},{8,24},{12,28},{16,0},{20,4},{24,8},{28,12},{1,17},{... | collective-permute-start | bytes 1572872 | tf_op jit(solution)/shard_map/ppermute | solution.py:11
  988.4 12.3 %collective-permute-start.23 = (f32[2,1,32,2048]{3,2,1,0:T(8,128)S(1)}, f32[2,1,32,2048]{3,2,1,0:T(8,128)S(1)}, u32[]{:S(2)}, u32[]{:S(2)}) collective-permute-start(f32[2,1,32,2048]{3,2,1,0:T(8,128)S(1)} %collective-permute-done.22), channel_id=1, source_target_pairs={{0,1},{1,0},{2,3},{3,2},{4,5},{5,4},{6,7},{7,6},{8,9},{9,8},{10,11... | collective-permute-start | bytes 1572872 | tf_op jit(solution)/shard_map/ppermute | solution.py:11
  1000.7 23.5 %collective-permute-start.24 = (f32[2,1,32,2048]{3,2,1,0:T(8,128)S(1)}, f32[2,1,32,2048]{3,2,1,0:T(8,128)S(1)}, u32[]{:S(2)}, u32[]{:S(2)}) collective-permute-start(f32[2,1,32,2048]{3,2,1,0:T(8,128)S(1)} %collective-permute-done.23), channel_id=1, source_target_pairs={{0,2},{1,3},{2,0},{3,1},{4,6},{5,7},{6,4},{7,5},{8,10},{9,11},{10,... | collective-permute-start | bytes 1572872 | tf_op jit(solution)/shard_map/ppermute | solution.py:11
  1072.0 15.9 %collective-permute-start.26 = (f32[1,32,32,1]{3,1,2,0:T(8,128)S(1)}, f32[1,32,32,1]{3,1,2,0:T(8,128)S(1)}, u32[]{:S(2)}, u32[]{:S(2)}) collective-permute-start(f32[1,32,32,1]{3,1,2,0:T(8,128)S(1)} %bitcast.338), channel_id=1, source_target_pairs={{1,0},{2,1},{3,2},{5,4},{6,5},{7,6},{9,8},{10,9},{11,10},{13,12},{... | collective-permute-start | bytes 12296 | tf_op jit(solution)/shard_map/ppermute | solution.py:17
  1074.5 15.5 %collective-permute-start.25 = (f32[1,32,1,64]{3,1,2,0:T(8,128)S(1)}, f32[1,32,1,64]{3,1,2,0:T(8,128)S(1)}, u32[]{:S(2)}, u32[]{:S(2)}) collective-permute-start(f32[1,32,1,64]{3,1,2,0:T(8,128)S(1)} %slice.232), channel_id=1, source_target_pairs={{4,0},{8,4},{12,8},{16,12},{20,16},{24,20},{28,24},{5,1},{9,5},{13... | collective-permute-start | bytes 24584 | tf_op jit(solution)/shard_map/ppermute | solution.py:17
  (19 other events, 66.7 us)
Sparse Core Ops, SparseCore 0:
  53.9 124.9 all-reduce.5
  310.3 125.6 all-reduce.7
  567.6 125.6 all-reduce.9
  825.0 125.6 all-reduce.11
where the time goes:
time: 1160 us; the launch traced here: 1150 us
  waiting for transfers between devices  774 us (67%)
  blocking collectives  193 us (17%)
  matrix products  65.3 us (6%)
  other arithmetic  40.8 us (4%)
  starting transfers between devices  35.6 us (3%)
  local copies, waits for them, and re-layouts  28.2 us (2%)
  between operations  14.8 us (1%)
    psum x4, waiting for transfers between devices, project(): return lax.psum(local_side, ('gx', 'gy'))  502 us
    ppermute x25, waiting for transfers between devices, swapped(): lax.ppermute(x, axis, [(i, i ^ 1 << apart) for i in range(lax.axis_size(a...  259 us
    psum x4, blocking collectives, body(): gram = lax.psum(gram_of(grown), ('gx', 'gy'))  152 us
    psum x1, blocking collectives, body(): lax.psum((local_terms[0], local_terms[1], local_terms[2], local_terms[3])...  40.9 us
    ppermute x25, starting transfers between devices, swapped(): lax.ppermute(x, axis, [(i, i ^ 1 << apart) for i in range(lax.axis_size(a...  32.9 us
  transfers between devices with their start and end apart: 31, of which 30 were waited for; matrix products, arithmetic and copies ran while one was open for 1% of the time, Pallas kernels for 0%

commit v1 on v0

--- a/solution.py
+++ b/solution.py
@@ -34,7 +34,8 @@
 
 
 def project(local_side):
-    return lax.psum(local_side, ("gx", "gy"))
+    find_tracks_now = lambda xs: lax.psum(lax.psum(xs, axis_name="gy"), axis_name="gx")
+    return find_tracks_now(local_side)
 
 
 def gram_of(grown):

time: 1160 us -> 1030 us (0.89)
  waiting for transfers between devices: 774 us -> 638 us
    psum x4 -> x8, waiting for transfers between devices: 502 us -> 366 us  [the longest x4 224 us: project(): lax.psum(lax.psum(xs, axis_name='gy'), axis_name='gx')]
  transfers between devices with their start and end apart: 31 -> 35, of which waited for: 30 -> 34; matrix products, arithmetic and copies ran while one was open for 1% -> 1% of each run, Pallas kernels for 0% -> 0%
where the time goes in v1:
time: 1030 us; the launch traced here: 1020 us
  waiting for transfers between devices  638 us (62%)
  blocking collectives  197 us (19%)
  matrix products  65.3 us (6%)
  other arithmetic  40.8 us (4%)
  starting transfers between devices  34.5 us (3%)
  local copies, waits for them, and re-layouts  28.2 us (3%)
  between operations  15.2 us (1%)
    ppermute x25, waiting for transfers between devices, swapped(): lax.ppermute(x, axis, [(i, i ^ 1 << apart) for i in range(lax.axis_size(a...  260 us
    psum x4, waiting for transfers between devices, project(): lax.psum(lax.psum(xs, axis_name='gy'), axis_name='gx')  224 us
    psum x4, blocking collectives, body(): gram = lax.psum(gram_of(grown), ('gx', 'gy'))  156 us
    psum x4, waiting for transfers between devices, project(): lax.psum(xs, axis_name='gy')  142 us
    psum x1, blocking collectives, body(): lax.psum((local_terms[0], local_terms[1], local_terms[2], local_terms[3])...  41 us
    ppermute x25, starting transfers between devices, swapped(): lax.ppermute(x, axis, [(i, i ^ 1 << apart) for i in range(lax.axis_size(a...  31.7 us
  transfers between devices with their start and end apart: 35, of which 34 were waited for; matrix products, arithmetic and copies ran while one was open for 1% of the time, Pallas kernels for 0%

profile of v1, /device:TPU:0, one launch (start us, length us, event | category | flops | bytes accessed | tf_op | source)
XLA Modules:
  0.0 1018.3 jit_solution(3443632294313039356)
XLA Ops:
  53.8 35.3 %all-reduce.10.cloned.1.call-done = f32[1,32,1024]{2,1,0:T(8,128)} async-done(((f32[1,32,1024]{2,1,0:T(8,128)}), f32[1,32,1024]{2,1,0:T(8,128)}) %all-reduce.10.cloned.1.call-update) | async-done | bytes 131088 | tf_op jit(solution)/shard_map/psum | solution.py:37
  89.2 56.1 %all-reduce.12.cloned.1.call-done = f32[1,32,1024]{2,1,0:T(8,128)} async-done(((f32[1,32,1024]{2,1,0:T(8,128)}), f32[1,32,1024]{2,1,0:T(8,128)}) %all-reduce.12.cloned.1.call-update) | async-done | bytes 131088 | tf_op jit(solution)/shard_map/psum | solution.py:37
  156.8 13.1 %collective-permute-done.6 = f32[2,1,32,2048]{3,2,1,0:T(8,128)S(1)} collective-permute-done((f32[2,1,32,2048]{3,2,1,0:T(8,128)S(1)}, f32[2,1,32,2048]{3,2,1,0:T(8,128)S(1)}, u32[]{:S(2)}, u32[]{:S(2)}) %collective-permute-start.6) | collective-permute-done | bytes 524320 | tf_op jit(solution)/shard_map/ppermute | solution.py:11
  170.8 12.3 %collective-permute-done.7 = f32[2,1,32,2048]{3,2,1,0:T(8,128)S(1)} collective-permute-done((f32[2,1,32,2048]{3,2,1,0:T(8,128)S(1)}, f32[2,1,32,2048]{3,2,1,0:T(8,128)S(1)}, u32[]{:S(2)}, u32[]{:S(2)}) %collective-permute-start.7) | collective-permute-done | bytes 524320 | tf_op jit(solution)/shard_map/ppermute | solution.py:11
  197.7 21.1 %collective-permute-done.9 = f32[2,1,32,2048]{3,2,1,0:T(8,128)S(1)} collective-permute-done((f32[2,1,32,2048]{3,2,1,0:T(8,128)S(1)}, f32[2,1,32,2048]{3,2,1,0:T(8,128)S(1)}, u32[]{:S(2)}, u32[]{:S(2)}) %collective-permute-start.9) | collective-permute-done | bytes 524320 | tf_op jit(solution)/shard_map/ppermute | solution.py:11
  225.8 38.9 %psum.114 = f32[1,32,32]{1,2,0:T(8,128)S(1)} all-reduce(f32[1,32,32]{1,2,0:T(8,128)S(1)} %convolution_bitcast_fusion.10), channel_id=1, replica_groups=mesh['gx'=8,'gy'=4] {'gx','gy'}, use_global_device_ids=true, to_apply=%region_2.3 | all-reduce | flops 1024 | bytes 8192 | tf_op jit(solution)/shard_map/psum | solution.py:119
  277.6 35.5 %all-reduce.14.cloned.1.call-done = f32[1,32,1024]{2,1,0:T(8,128)} async-done(((f32[1,32,1024]{2,1,0:T(8,128)}), f32[1,32,1024]{2,1,0:T(8,128)}) %all-reduce.14.cloned.1.call-update) | async-done | bytes 131088 | tf_op jit(solution)/shard_map/psum | solution.py:37
  313.1 56.0 %all-reduce.16.cloned.1.call-done = f32[1,32,1024]{2,1,0:T(8,128)} async-done(((f32[1,32,1024]{2,1,0:T(8,128)}), f32[1,32,1024]{2,1,0:T(8,128)}) %all-reduce.16.cloned.1.call-update) | async-done | bytes 131088 | tf_op jit(solution)/shard_map/psum | solution.py:37
  380.6 13.1 %collective-permute-done.11 = f32[2,1,32,2048]{3,2,1,0:T(8,128)S(1)} collective-permute-done((f32[2,1,32,2048]{3,2,1,0:T(8,128)S(1)}, f32[2,1,32,2048]{3,2,1,0:T(8,128)S(1)}, u32[]{:S(2)}, u32[]{:S(2)}) %collective-permute-start.11) | collective-permute-done | bytes 524320 | tf_op jit(solution)/shard_map/ppermute | solution.py:11
  394.6 12.3 %collective-permute-done.12 = f32[2,1,32,2048]{3,2,1,0:T(8,128)S(1)} collective-permute-done((f32[2,1,32,2048]{3,2,1,0:T(8,128)S(1)}, f32[2,1,32,2048]{3,2,1,0:T(8,128)S(1)}, u32[]{:S(2)}, u32[]{:S(2)}) %collective-permute-start.12) | collective-permute-done | bytes 524320 | tf_op jit(solution)/shard_map/ppermute | solution.py:11
  421.5 21.1 %collective-permute-done.14 = f32[2,1,32,2048]{3,2,1,0:T(8,128)S(1)} collective-permute-done((f32[2,1,32,2048]{3,2,1,0:T(8,128)S(1)}, f32[2,1,32,2048]{3,2,1,0:T(8,128)S(1)}, u32[]{:S(2)}, u32[]{:S(2)}) %collective-permute-start.14) | collective-permute-done | bytes 524320 | tf_op jit(solution)/shard_map/ppermute | solution.py:11
  449.6 38.9 %psum.117 = f32[1,32,32]{1,2,0:T(8,128)S(1)} all-reduce(f32[1,32,32]{1,2,0:T(8,128)S(1)} %convolution_bitcast_fusion.9), channel_id=1, replica_groups=mesh['gx'=8,'gy'=4] {'gx','gy'}, use_global_device_ids=true, to_apply=%region_7.10 | all-reduce | flops 1024 | bytes 8192 | tf_op jit(solution)/shard_map/psum | solution.py:119
  501.4 35.5 %all-reduce.18.cloned.1.call-done = f32[1,32,1024]{2,1,0:T(8,128)} async-done(((f32[1,32,1024]{2,1,0:T(8,128)}), f32[1,32,1024]{2,1,0:T(8,128)}) %all-reduce.18.cloned.1.call-update) | async-done | bytes 131088 | tf_op jit(solution)/shard_map/psum | solution.py:37
  536.9 56.0 %all-reduce.20.cloned.1.call-done = f32[1,32,1024]{2,1,0:T(8,128)} async-done(((f32[1,32,1024]{2,1,0:T(8,128)}), f32[1,32,1024]{2,1,0:T(8,128)}) %all-reduce.20.cloned.1.call-update) | async-done | bytes 131088 | tf_op jit(solution)/shard_map/psum | solution.py:37
  604.4 13.1 %collective-permute-done.16 = f32[2,1,32,2048]{3,2,1,0:T(8,128)S(1)} collective-permute-done((f32[2,1,32,2048]{3,2,1,0:T(8,128)S(1)}, f32[2,1,32,2048]{3,2,1,0:T(8,128)S(1)}, u32[]{:S(2)}, u32[]{:S(2)}) %collective-permute-start.16) | collective-permute-done | bytes 524320 | tf_op jit(solution)/shard_map/ppermute | solution.py:11
  618.4 12.3 %collective-permute-done.17 = f32[2,1,32,2048]{3,2,1,0:T(8,128)S(1)} collective-permute-done((f32[2,1,32,2048]{3,2,1,0:T(8,128)S(1)}, f32[2,1,32,2048]{3,2,1,0:T(8,128)S(1)}, u32[]{:S(2)}, u32[]{:S(2)}) %collective-permute-start.17) | collective-permute-done | bytes 524320 | tf_op jit(solution)/shard_map/ppermute | solution.py:11
  645.3 21.1 %collective-permute-done.19 = f32[2,1,32,2048]{3,2,1,0:T(8,128)S(1)} collective-permute-done((f32[2,1,32,2048]{3,2,1,0:T(8,128)S(1)}, f32[2,1,32,2048]{3,2,1,0:T(8,128)S(1)}, u32[]{:S(2)}, u32[]{:S(2)}) %collective-permute-start.19) | collective-permute-done | bytes 524320 | tf_op jit(solution)/shard_map/ppermute | solution.py:11
  673.4 39.1 %psum.120 = f32[1,32,32]{1,2,0:T(8,128)S(1)} all-reduce(f32[1,32,32]{1,2,0:T(8,128)S(1)} %convolution_bitcast_fusion.8), channel_id=1, replica_groups=mesh['gx'=8,'gy'=4] {'gx','gy'}, use_global_device_ids=true, to_apply=%region_10.13 | all-reduce | flops 1024 | bytes 8192 | tf_op jit(solution)/shard_map/psum | solution.py:119
  725.4 35.5 %all-reduce.22.cloned.1.call-done = f32[1,32,1024]{2,1,0:T(8,128)} async-done(((f32[1,32,1024]{2,1,0:T(8,128)}), f32[1,32,1024]{2,1,0:T(8,128)}) %all-reduce.22.cloned.1.call-update) | async-done | bytes 131088 | tf_op jit(solution)/shard_map/psum | solution.py:37
  760.9 56.2 %all-reduce.24.cloned.1.call-done = f32[1,32,1024]{2,1,0:T(8,128)} async-done(((f32[1,32,1024]{2,1,0:T(8,128)}), f32[1,32,1024]{2,1,0:T(8,128)}) %all-reduce.24.cloned.1.call-update) | async-done | bytes 131088 | tf_op jit(solution)/shard_map/psum | solution.py:37
  828.6 13.1 %collective-permute-done.21 = f32[2,1,32,2048]{3,2,1,0:T(8,128)S(1)} collective-permute-done((f32[2,1,32,2048]{3,2,1,0:T(8,128)S(1)}, f32[2,1,32,2048]{3,2,1,0:T(8,128)S(1)}, u32[]{:S(2)}, u32[]{:S(2)}) %collective-permute-start.21) | collective-permute-done | bytes 524320 | tf_op jit(solution)/shard_map/ppermute | solution.py:11
  869.5 21.1 %collective-permute-done.24 = f32[2,1,32,2048]{3,2,1,0:T(8,128)S(1)} collective-permute-done((f32[2,1,32,2048]{3,2,1,0:T(8,128)S(1)}, f32[2,1,32,2048]{3,2,1,0:T(8,128)S(1)}, u32[]{:S(2)}, u32[]{:S(2)}) %collective-permute-start.24) | collective-permute-done | bytes 524320 | tf_op jit(solution)/shard_map/ppermute | solution.py:11
  892.5 38.9 %psum.123 = f32[1,32,32]{1,2,0:T(8,128)S(1)} all-reduce(f32[1,32,32]{1,2,0:T(8,128)S(1)} %convolution_bitcast_fusion.7), channel_id=1, replica_groups=mesh['gx'=8,'gy'=4] {'gx','gy'}, use_global_device_ids=true, to_apply=%region_13.16 | all-reduce | flops 1024 | bytes 8192 | tf_op jit(solution)/shard_map/psum | solution.py:119
  957.8 41.0 %all-reduce = (f32[1,1,32,32]{2,3,1,0:T(8,128)S(1)}, f32[1,1,32,32]{2,3,1,0:T(8,128)S(1)}, f32[1,1,32,32]{3,2,1,0:T(8,128)S(1)}, f32[1,1,32,32]{3,2,1,0:T(8,128)S(1)}) all-reduce(f32[1,1,32,32]{2,3,1,0:T(8,128)S(1)} %convolution_bitcast_fusion.5, ...), channel_id=1, replica_groups=mesh['gx'=8,'gy'=4] {'gx','gy'}, use_global_device_ids=true, to_apply=%region_14.17 | all-reduce | flops 4096 | bytes 32768 | tf_op jit(solution)/shard_map/psum | solution.py:125
  (227 shorter events, 266.7 us)
Async XLA Ops:
  7.2 81.9 %all-reduce.10.cloned.1.call-start = ((), (), s32[]{:S(2)}) async-start(), calls=%async_computation | async-start | bytes 262144 | tf_op jit(solution)/shard_map/psum | solution.py:37
  34.3 12.6 %collective-permute-start.4 = (f32[1,1,32,2048]{3,2,1,0:T(8,128)S(1)}, f32[1,1,32,2048]{3,2,1,0:T(8,128)S(1)}, u32[]{:S(2)}, u32[]{:S(2)}) collective-permute-start(f32[1,1,32,2048]{3,2,1,0:T(8,128)S(1)} %collective-permute-done.3), channel_id=1, source_target_pairs={{0,2},{1,3},{2,0},{3,1},{4,6},{5,7},{6,4},{7,5},{8,10},{9,11},{10,... | collective-permute-start | bytes 786440 | tf_op jit(solution)/shard_map/ppermute | solution.py:11
  53.8 91.5 %all-reduce.12.cloned.1.call-start = ((), (), s32[]{:S(2)}) async-start(), calls=%async_computation.1 | async-start | bytes 262144 | tf_op jit(solution)/shard_map/psum | solution.py:37
  89.1 223.9 %all-reduce.14.cloned.1.call-start = ((), (), s32[]{:S(2)}) async-start(), calls=%async_computation.2 | async-start | bytes 262144 | tf_op jit(solution)/shard_map/psum | solution.py:37
  155.9 14.0 %collective-permute-start.6 = (f32[2,1,32,2048]{3,2,1,0:T(8,128)S(1)}, f32[2,1,32,2048]{3,2,1,0:T(8,128)S(1)}, u32[]{:S(2)}, u32[]{:S(2)}) collective-permute-start(f32[2,1,32,2048]{3,2,1,0:T(8,128)S(1)} %collective-permute-done.5), channel_id=1, source_target_pairs={{0,8},{4,12},{8,0},{12,4},{16,24},{20,28},{24,16},{28,20},{1,9},{5... | collective-permute-start | bytes 1572872 | tf_op jit(solution)/shard_map/ppermute | solution.py:11
  169.9 13.1 %collective-permute-start.7 = (f32[2,1,32,2048]{3,2,1,0:T(8,128)S(1)}, f32[2,1,32,2048]{3,2,1,0:T(8,128)S(1)}, u32[]{:S(2)}, u32[]{:S(2)}) collective-permute-start(f32[2,1,32,2048]{3,2,1,0:T(8,128)S(1)} %collective-permute-done.6), channel_id=1, source_target_pairs={{0,16},{4,20},{8,24},{12,28},{16,0},{20,4},{24,8},{28,12},{1,17},{... | collective-permute-start | bytes 1572872 | tf_op jit(solution)/shard_map/ppermute | solution.py:11
  195.3 23.5 %collective-permute-start.9 = (f32[2,1,32,2048]{3,2,1,0:T(8,128)S(1)}, f32[2,1,32,2048]{3,2,1,0:T(8,128)S(1)}, u32[]{:S(2)}, u32[]{:S(2)}) collective-permute-start(f32[2,1,32,2048]{3,2,1,0:T(8,128)S(1)} %collective-permute-done.8), channel_id=1, source_target_pairs={{0,2},{1,3},{2,0},{3,1},{4,6},{5,7},{6,4},{7,5},{8,10},{9,11},{10,... | collective-permute-start | bytes 1572872 | tf_op jit(solution)/shard_map/ppermute | solution.py:11
  277.5 91.6 %all-reduce.16.cloned.1.call-start = ((), (), s32[]{:S(2)}) async-start(), calls=%async_computation.3 | async-start | bytes 262144 | tf_op jit(solution)/shard_map/psum | solution.py:37
  313.1 223.8 %all-reduce.18.cloned.1.call-start = ((), (), s32[]{:S(2)}) async-start(), calls=%async_computation.4 | async-start | bytes 262144 | tf_op jit(solution)/shard_map/psum | solution.py:37
  379.7 14.0 %collective-permute-start.11 = (f32[2,1,32,2048]{3,2,1,0:T(8,128)S(1)}, f32[2,1,32,2048]{3,2,1,0:T(8,128)S(1)}, u32[]{:S(2)}, u32[]{:S(2)}) collective-permute-start(f32[2,1,32,2048]{3,2,1,0:T(8,128)S(1)} %collective-permute-done.10), channel_id=1, source_target_pairs={{0,8},{4,12},{8,0},{12,4},{16,24},{20,28},{24,16},{28,20},{1,9},{5... | collective-permute-start | bytes 1572872 | tf_op jit(solution)/shard_map/ppermute | solution.py:11
  393.7 13.1 %collective-permute-start.12 = (f32[2,1,32,2048]{3,2,1,0:T(8,128)S(1)}, f32[2,1,32,2048]{3,2,1,0:T(8,128)S(1)}, u32[]{:S(2)}, u32[]{:S(2)}) collective-permute-start(f32[2,1,32,2048]{3,2,1,0:T(8,128)S(1)} %collective-permute-done.11), channel_id=1, source_target_pairs={{0,16},{4,20},{8,24},{12,28},{16,0},{20,4},{24,8},{28,12},{1,17},{... | collective-permute-start | bytes 1572872 | tf_op jit(solution)/shard_map/ppermute | solution.py:11
  406.8 12.3 %collective-permute-start.13 = (f32[2,1,32,2048]{3,2,1,0:T(8,128)S(1)}, f32[2,1,32,2048]{3,2,1,0:T(8,128)S(1)}, u32[]{:S(2)}, u32[]{:S(2)}) collective-permute-start(f32[2,1,32,2048]{3,2,1,0:T(8,128)S(1)} %collective-permute-done.12), channel_id=1, source_target_pairs={{0,1},{1,0},{2,3},{3,2},{4,5},{5,4},{6,7},{7,6},{8,9},{9,8},{10,11... | collective-permute-start | bytes 1572872 | tf_op jit(solution)/shard_map/ppermute | solution.py:11
  419.1 23.5 %collective-permute-start.14 = (f32[2,1,32,2048]{3,2,1,0:T(8,128)S(1)}, f32[2,1,32,2048]{3,2,1,0:T(8,128)S(1)}, u32[]{:S(2)}, u32[]{:S(2)}) collective-permute-start(f32[2,1,32,2048]{3,2,1,0:T(8,128)S(1)} %collective-permute-done.13), channel_id=1, source_target_pairs={{0,2},{1,3},{2,0},{3,1},{4,6},{5,7},{6,4},{7,5},{8,10},{9,11},{10,... | collective-permute-start | bytes 1572872 | tf_op jit(solution)/shard_map/ppermute | solution.py:11
  501.3 91.6 %all-reduce.20.cloned.1.call-start = ((), (), s32[]{:S(2)}) async-start(), calls=%async_computation.5 | async-start | bytes 262144 | tf_op jit(solution)/shard_map/psum | solution.py:37
  536.9 224.0 %all-reduce.22.cloned.1.call-start = ((), (), s32[]{:S(2)}) async-start(), calls=%async_computation.6 | async-start | bytes 262144 | tf_op jit(solution)/shard_map/psum | solution.py:37
  603.6 14.0 %collective-permute-start.16 = (f32[2,1,32,2048]{3,2,1,0:T(8,128)S(1)}, f32[2,1,32,2048]{3,2,1,0:T(8,128)S(1)}, u32[]{:S(2)}, u32[]{:S(2)}) collective-permute-start(f32[2,1,32,2048]{3,2,1,0:T(8,128)S(1)} %collective-permute-done.15), channel_id=1, source_target_pairs={{0,8},{4,12},{8,0},{12,4},{16,24},{20,28},{24,16},{28,20},{1,9},{5... | collective-permute-start | bytes 1572872 | tf_op jit(solution)/shard_map/ppermute | solution.py:11
  617.5 13.1 %collective-permute-start.17 = (f32[2,1,32,2048]{3,2,1,0:T(8,128)S(1)}, f32[2,1,32,2048]{3,2,1,0:T(8,128)S(1)}, u32[]{:S(2)}, u32[]{:S(2)}) collective-permute-start(f32[2,1,32,2048]{3,2,1,0:T(8,128)S(1)} %collective-permute-done.16), channel_id=1, source_target_pairs={{0,16},{4,20},{8,24},{12,28},{16,0},{20,4},{24,8},{28,12},{1,17},{... | collective-permute-start | bytes 1572872 | tf_op jit(solution)/shard_map/ppermute | solution.py:11
  642.9 23.5 %collective-permute-start.19 = (f32[2,1,32,2048]{3,2,1,0:T(8,128)S(1)}, f32[2,1,32,2048]{3,2,1,0:T(8,128)S(1)}, u32[]{:S(2)}, u32[]{:S(2)}) collective-permute-start(f32[2,1,32,2048]{3,2,1,0:T(8,128)S(1)} %collective-permute-done.18), channel_id=1, source_target_pairs={{0,2},{1,3},{2,0},{3,1},{4,6},{5,7},{6,4},{7,5},{8,10},{9,11},{10,... | collective-permute-start | bytes 1572872 | tf_op jit(solution)/shard_map/ppermute | solution.py:11
  725.4 91.7 %all-reduce.24.cloned.1.call-start = ((), (), s32[]{:S(2)}) async-start(), calls=%async_computation.7 | async-start | bytes 262144 | tf_op jit(solution)/shard_map/psum | solution.py:37
  827.7 14.0 %collective-permute-start.21 = (f32[2,1,32,2048]{3,2,1,0:T(8,128)S(1)}, f32[2,1,32,2048]{3,2,1,0:T(8,128)S(1)}, u32[]{:S(2)}, u32[]{:S(2)}) collective-permute-start(f32[2,1,32,2048]{3,2,1,0:T(8,128)S(1)} %collective-permute-done.20), channel_id=1, source_target_pairs={{0,8},{4,12},{8,0},{12,4},{16,24},{20,28},{24,16},{28,20},{1,9},{5... | collective-permute-start | bytes 1572872 | tf_op jit(solution)/shard_map/ppermute | solution.py:11
  841.7 13.1 %collective-permute-start.22 = (f32[2,1,32,2048]{3,2,1,0:T(8,128)S(1)}, f32[2,1,32,2048]{3,2,1,0:T(8,128)S(1)}, u32[]{:S(2)}, u32[]{:S(2)}) collective-permute-start(f32[2,1,32,2048]{3,2,1,0:T(8,128)S(1)} %collective-permute-done.21), channel_id=1, source_target_pairs={{0,16},{4,20},{8,24},{12,28},{16,0},{20,4},{24,8},{28,12},{1,17},{... | collective-permute-start | bytes 1572872 | tf_op jit(solution)/shard_map/ppermute | solution.py:11
  867.1 23.5 %collective-permute-start.24 = (f32[2,1,32,2048]{3,2,1,0:T(8,128)S(1)}, f32[2,1,32,2048]{3,2,1,0:T(8,128)S(1)}, u32[]{:S(2)}, u32[]{:S(2)}) collective-permute-start(f32[2,1,32,2048]{3,2,1,0:T(8,128)S(1)} %collective-permute-done.23), channel_id=1, source_target_pairs={{0,2},{1,3},{2,0},{3,1},{4,6},{5,7},{6,4},{7,5},{8,10},{9,11},{10,... | collective-permute-start | bytes 1572872 | tf_op jit(solution)/shard_map/ppermute | solution.py:11
  939.3 15.1 %collective-permute-start.26 = (f32[1,32,32,1]{3,1,2,0:T(8,128)S(1)}, f32[1,32,32,1]{3,1,2,0:T(8,128)S(1)}, u32[]{:S(2)}, u32[]{:S(2)}) collective-permute-start(f32[1,32,32,1]{3,1,2,0:T(8,128)S(1)} %bitcast.338), channel_id=1, source_target_pairs={{1,0},{2,1},{3,2},{5,4},{6,5},{7,6},{9,8},{10,9},{11,10},{13,12},{... | collective-permute-start | bytes 12296 | tf_op jit(solution)/shard_map/ppermute | solution.py:17
  941.7 14.7 %collective-permute-start.25 = (f32[1,32,1,64]{3,1,2,0:T(8,128)S(1)}, f32[1,32,1,64]{3,1,2,0:T(8,128)S(1)}, u32[]{:S(2)}, u32[]{:S(2)}) collective-permute-start(f32[1,32,1,64]{3,1,2,0:T(8,128)S(1)} %slice.232), channel_id=1, source_target_pairs={{4,0},{8,4},{12,8},{16,12},{20,16},{24,20},{28,24},{5,1},{9,5},{13... | collective-permute-start | bytes 24584 | tf_op jit(solution)/shard_map/ppermute | solution.py:17
  (23 other events, 112.9 us)
Sparse Core Ops, SparseCore 0:
  53.9 35.1 all-reduce.9
  92.1 53.1 all-reduce.11
  277.6 35.3 all-reduce.13
  315.9 53.1 all-reduce.15
  501.5 35.3 all-reduce.17
  539.8 53.1 all-reduce.19
  725.5 35.3 all-reduce.21
  763.9 53.1 all-reduce.23
